TPU v7x, 32 devices: a whole 2x2x4 slice. The times are simulated.
32 devices in a mesh: node: 8 (over z, y), local: 4 (over x, core).
Axes of the slice: x: 2, y: 2, z: 4, core: 2. Of those that a mesh axis runs over, the one named last changes fastest.
Arguments:
- tokens: bfloat16 [4096, 7168], P(('node', 'local')), may hold values from -6 to 6
- w_gate: bfloat16 [8, 7168, 1024], P('node', None, 'local'), may hold values from -0.0625 to 0.0625
- w_up: bfloat16 [8, 7168, 1024], P('node', None, 'local'), may hold values from -0.0625 to 0.0625
- w_down: bfloat16 [8, 1024, 7168], P('node', 'local'), may hold values from -0.1875 to 0.1875
- chosen: int32 [8, 48], replicated, may hold values from 0 to 4095, as said below
- counts: int32 [8], replicated, may hold values from 3 to 48, as said below
- gates: float32 [8, 48], replicated, may hold values from 0.2 to 1
Outputs:
- mixed: bfloat16 [4096, 7168], P(('node', 'local'))
Inputs may be any that keep to these rules, and one draw needn't show every extreme that they name: `chosen`: each expert's list holds distinct tokens; in each list at most 3 entries lie in one device's block of 128 consecutive tokens, and for every expert some block holds exactly 3 live entries. `counts`: some expert has exactly 48 live entries.
All inputs are finite; a program needn't handle non-finite values.
Results may differ from a plain program's by a relative error of at most 0.014.
Values may be sent and summed in bfloat16 or wider, within the bound.
A program may use at most 128 MiB of HBM per device.

v0:
```python
import jax
import jax.numpy as jnp
from jax import lax
from jax.sharding import PartitionSpec as P

SLOT = 3


def shards(tokens, w_gate, w_up, w_down, chosen, counts, gates):
    tok_dev = tokens.shape[0]
    width = tokens.shape[1]
    n_node = lax.axis_size("node")
    n_local = lax.axis_size("local")
    devices = n_node * n_local
    cap = chosen.shape[1]
    experts = chosen.shape[0]
    myself = lax.axis_index("node") * n_local + lax.axis_index("local")
    live = jnp.arange(cap, dtype=jnp.int32)[None, :] < counts[:, None]
    owner = chosen // tok_dev
    mine = live & (owner == myself)
    rank = jnp.cumsum(mine.astype(jnp.int32), axis=1) - 1
    select = (
        mine[:, :, None] & (rank[:, :, None] == jnp.arange(SLOT, dtype=jnp.int32)[None, None, :])
    ).astype(jnp.int32)
    position = chosen - owner * tok_dev
    token_slot = jnp.sum(select * position[:, :, None], axis=1)
    present = jnp.sum(select, axis=1)
    outgoing = tokens[token_slot.reshape(-1)].reshape(experts, SLOT, width)
    outgoing = outgoing * present[:, :, None].astype(jnp.bfloat16)
    expert = lax.axis_index("node")
    picked = lax.dynamic_index_in_dim(chosen, expert, 0, keepdims=False)
    count = lax.dynamic_index_in_dim(counts, expert, 0, keepdims=False)
    weight = lax.dynamic_index_in_dim(gates, expert, 0, keepdims=False)
    valid = jnp.arange(cap, dtype=jnp.int32) < count
    holder = picked // tok_dev
    member = (
        (holder[:, None] == jnp.arange(devices, dtype=jnp.int32)[None, :]) & valid[:, None]
    ).astype(jnp.int32)
    order_in = jnp.sum(member * jnp.cumsum(member, axis=0), axis=1) - 1
    column = holder * SLOT + order_in
    table = jnp.sum(
        jnp.where(
            valid[:, None]
            & (column[:, None] == jnp.arange(devices * SLOT, dtype=jnp.int32)[None, :]),
            weight[:, None],
            jnp.float32(0.0),
        ),
        axis=0,
    )
    table = table.reshape(n_node, n_local, SLOT).transpose(1, 0, 2)
    gate_mat = w_gate[0]
    up_mat = w_up[0]
    down_mat = w_down[0]
    ff_dev = gate_mat.shape[1]
    arrived = lax.all_to_all(outgoing, "node", split_axis=0, concat_axis=0, tiled=True)
    piece = lax.all_gather(arrived[None], "local", axis=0, tiled=True)
    flat = piece.reshape(-1, width)
    gate_val = jnp.dot(flat, gate_mat, preferred_element_type=jnp.float32)
    up_val = jnp.dot(flat, up_mat, preferred_element_type=jnp.float32)
    hidden = (jax.nn.silu(gate_val) * up_val).astype(jnp.bfloat16)
    down_hidden = hidden.reshape(piece.shape[0], n_node, SLOT, ff_dev)
    count_rows = down_hidden.shape[0]
    down_val = jnp.dot(
        down_hidden.reshape(-1, ff_dev), down_mat, preferred_element_type=jnp.float32
    )
    down_val = down_val.reshape(count_rows, n_node, SLOT, width)
    partial_value = (down_val * table[:, :, :, None]).astype(jnp.bfloat16)
    summed = lax.psum_scatter(
        partial_value.astype(jnp.float32).astype(jnp.bfloat16),
        "local",
        scatter_dimension=0,
        tiled=True,
    )
    returned = lax.all_to_all(summed, "node", split_axis=1, concat_axis=1, tiled=True)
    answers = returned[0].reshape(experts * SLOT, width)
    placing = (jnp.arange(tok_dev, dtype=jnp.int32)[:, None] == token_slot.reshape(-1)[None, :]) & (
        present.reshape(-1)[None, :] > 0
    )
    mixed = jnp.dot(placing.astype(jnp.bfloat16), answers, preferred_element_type=jnp.float32)
    return mixed.astype(jnp.bfloat16)


def solution(mesh):
    in_specs = (
        P(("node", "local"), None),
        P("node", None, "local"),
        P("node", None, "local"),
        P("node", "local", None),
        P(),
        P(),
        P(),
    )
    out_specs = P(("node", "local"), None)
    return jax.shard_map(shards, mesh=mesh, in_specs=in_specs, out_specs=out_specs, check_vma=False)
```

profile of v0, /device:TPU:0, one launch (start us, length us, event | category | flops | bytes accessed | tf_op | source)
XLA Modules:
  0.0 119.9 jit_solution(16415027315541604071)
XLA Ops:
  6.5 0.9 fusion.25
  7.6 0.7 multiply_subtract_fusion
  8.7 0.8 gather_fusion
  9.8 0.3 broadcast_multiply_fusion
  10.1 20.3 %all_to_all.10 = bf16[8,3,7168]{2,1,0:T(4,128)(2,1)S(1)} all-to-all(bf16[8,3,7168]{2,1,0:T(4,128)(2,1)S(1)} %broadcast_multiply_fusion), channel_id=1, replica_groups=mesh['node'=8,'local'=4] {'node'}, dimensions={0} | all-to-all | bytes 688128 | tf_op jit(solution)/shard_map/all_to_all | solution.py:55
  30.4 0.9 copy.22
  31.3 0.6 dynamic_slice.12
  32.0 0.7 and_select_fusion
  32.6 0.6 iota_compare_fusion.5
  33.5 0.7 dynamic-slice_bitcast_fusion
  34.3 0.7 add_add_fusion
  35.4 13.7 %all-gather.3.cloned.1.call-done = bf16[32,3,7168]{2,0,1:T(8,128)(2,1)} async-done(((bf16[8,3,7168]{2,0,1:T(8,128)(2,1)}), bf16[32,3,7168]{2,0,1:T(8,128)(2,1)}) %all-gather.3.cloned.1.call-update) | async-done | bytes 1376272 | tf_op jit(solution)/shard_map/all_gather | solution.py:56
  49.0 3.7 %copy.23 = bf16[32,3,7168]{2,1,0:T(4,128)(2,1)} copy(bf16[32,3,7168]{2,0,1:T(8,128)(2,1)} %all-gather.3.cloned.1.call-done) | data formatting | bytes 2752512 | tf_op jit(solution)/shard_map/all_gather | solution.py:56
  52.8 3.0 %reshape.117 = bf16[96,7168]{1,0:T(8,128)(2,1)S(1)} reshape(bf16[32,3,7168]{2,1,0:T(4,128)(2,1)} %copy.23) | data formatting | bytes 2752512 | tf_op jit(solution)/shard_map/reshape | solution.py:57
  55.8 2.9 %fusion.4 = f32[96,256]{1,0:T(8,128)S(1)} fusion(bf16[96,7168]{1,0:T(8,128)(2,1)S(1)} %reshape.117, bf16[1,7168,256]{2,1,0:T(8,128)(2,1)} %param.8), kind=kOutput, calls=%fused_computation.7 | convolution fusion | flops 352321536 | bytes 5144576 | tf_op jit(solution)/shard_map/dot_general | solution.py:58
  58.7 0.2 copy-done.1
  58.9 0.7 fusion.9
  59.7 3.8 %fusion = bf16[4,8,3,7168]{3,1,2,0:T(8,128)(2,1)} fusion(bf16[1,256,7168]{2,1,0:T(8,128)(2,1)} %param.10, f32[4,8,3]{1,2,0:T(4,128)S(1)} %copy.25, bf16[4,8,3,256]{3,2,1,0:T(4,128)(2,1)S(1)} %dot_general.16), kind=kOutput, calls=%fused_computation.3 | convolution fusion | flops 353697792 | bytes 5095808 | tf_op jit(solution)/shard_map/dot_general | solution.py:63
  63.6 26.9 %reduce-scatter.2.cloned.1.call-done = bf16[1,8,3,7168]{3,1,2,0:T(8,128)(2,1)} async-done(((bf16[4,8,3,7168]{3,1,2,0:T(8,128)(2,1)}), bf16[1,8,3,7168]{3,1,2,0:T(8,128)(2,1)}) %reduce-scatter.2.cloned.1.call-update) | async-done | bytes 344080 | tf_op jit(solution)/shard_map/reduce_scatter | solution.py:68
  90.4 2.0 %copy.26 = bf16[1,8,3,7168]{3,2,0,1:T(4,128)(2,1)} copy(bf16[1,8,3,7168]{3,1,2,0:T(8,128)(2,1)} %reduce-scatter.2.cloned.1.call-done) | data formatting | bytes 688128 | tf_op jit(solution)/shard_map/reduce_scatter | solution.py:68
  92.5 5.5 %all-to-all-start.1 = ((bf16[1,8,3,7168]{3,2,0,1:T(4,128)(2,1)}), bf16[1,8,3,7168]{3,2,0,1:T(4,128)(2,1)S(1)}, u32[]{:S(2)}, u32[]{:S(2)}) async-start(bf16[1,8,3,7168]{3,2,0,1:T(4,128)(2,1)} %copy.26), calls=%async_computation.2 | async-start | bytes 917504 | tf_op jit(solution)/shard_map/all_to_all | solution.py:74
  98.3 12.7 %all-to-all-done.1 = bf16[1,8,3,7168]{3,2,0,1:T(4,128)(2,1)S(1)} async-done(((bf16[1,8,3,7168]{3,2,0,1:T(4,128)(2,1)}), bf16[1,8,3,7168]{3,2,0,1:T(4,128)(2,1)S(1)}, u32[]{:S(2)}, u32[]{:S(2)}) %all-to-all-start.1) | async-done | bytes 344096 | tf_op jit(solution)/shard_map/all_to_all | solution.py:74
  110.9 0.3 reshape_squeeze.3
  111.2 1.9 %convolution_convert_fusion = bf16[128,7168]{1,0:T(8,128)(2,1)} fusion(bf16[24,7168]{1,0:T(8,128)(2,1)S(1)} %reshape_squeeze.3, s32[24]{0:T(128)S(1)} %eq.66, pred[24]{0:T(512)(128)(4,1)S(1)} %gt.12), kind=kOutput, calls=%fused_computation.1 | convolution fusion | flops 44963840 | bytes 2179192 | tf_op jit(solution)/shard_map/dot_general | solution.py:79
  (29 shorter events, 1.9 us)
Async XLA Ops:
  6.5 2.2 %copy-start = (bf16[128,7168]{1,0:T(8,128)(2,1)S(1)}, bf16[128,7168]{1,0:T(8,128)(2,1)}, u32[]{:S(2)}) copy-start(bf16[128,7168]{1,0:T(8,128)(2,1)} %param.7) | copy-start | bytes 5505028
  6.5 42.5 %all-gather.3.cloned.1.call-start = ((), (), s32[]{:S(2)}) async-start(), calls=%async_computation.4 | async-start | bytes 1720320 | tf_op jit(solution)/shard_map/all_gather | solution.py:56
  8.7 22.6 %copy-start.2 = (s32[8]{0:T(128)S(1)}, s32[8]{0:T(128)}, u32[]{:S(2)}) copy-start(s32[8]{0:T(128)} %param.12) | copy-start | bytes 100
  31.3 59.2 %reduce-scatter.2.cloned.1.call-start = ((), (), s32[]{:S(2)}) async-start(), calls=%async_computation.3 | async-start | bytes 1720320 | tf_op jit(solution)/shard_map/reduce_scatter | solution.py:68
  55.8 3.1 %copy-start.1 = (bf16[1,7168,256]{2,1,0:T(8,128)(2,1)S(1)}, bf16[1,7168,256]{2,1,0:T(8,128)(2,1)}, u32[]{:S(2)}) copy-start(bf16[1,7168,256]{2,1,0:T(8,128)(2,1)} %param.9) | copy-start | bytes 11010052
  92.5 18.4 %all-to-all-start.1 = ((bf16[1,8,3,7168]{3,2,0,1:T(4,128)(2,1)}), bf16[1,8,3,7168]{3,2,0,1:T(4,128)(2,1)S(1)}, u32[]{:S(2)}, u32[]{:S(2)}) async-start(bf16[1,8,3,7168]{3,2,0,1:T(4,128)(2,1)} %copy.26), calls=%async_computation.2 | async-start | bytes 917504 | tf_op jit(solution)/shard_map/all_to_all | solution.py:74
Sparse Core Ops, SparseCore 0:
  31.4 17.5 all-gather.2
  63.7 26.7 reduce-scatter.1
where the time goes:
time: 120 us
  waiting for transfers between devices  53.3 us (44%)
  blocking collectives  20.3 us (17%)
  between operations  13.5 us (11%)
  local copies, waits for them, and re-layouts  13.2 us (11%)
  matrix products  9.34 us (8%)
  starting transfers between devices  5.55 us (5%)
  other arithmetic  4.75 us (4%)
    reduce_scatter x1, waiting for transfers between devices, shards(): lax.psum_scatter(partial_value.astype(jnp.float32).astype(jnp.bfloat16),...  26.9 us
    all_to_all x1, blocking collectives, shards(): lax.all_to_all(outgoing, 'node', split_axis=0, concat_axis=0, tiled=True)  20.3 us
    all_gather x1, waiting for transfers between devices, shards(): piece = lax.all_gather(arrived[None], 'local', axis=0, tiled=True)  13.7 us
    all_to_all x1, waiting for transfers between devices, shards(): lax.all_to_all(summed, 'node', split_axis=1, concat_axis=1, tiled=True)  12.7 us
    all_to_all x1, starting transfers between devices, shards(): lax.all_to_all(summed, 'node', split_axis=1, concat_axis=1, tiled=True)  5.51 us
    dot_general x1, matrix products, shards(): jnp.dot(down_hidden.reshape(-1, ff_dev), down_mat, preferred_element_type...  3.84 us
    all_gather x1, local copies, waits for them, and re-layouts, shards(): piece = lax.all_gather(arrived[None], 'local', axis=0, tiled=True)  3.75 us
    reshape x1, local copies, waits for them, and re-layouts, shards(): flat = piece.reshape(-1, width)  2.97 us
  transfers between devices with their start and end apart: 3, of which 3 were waited for; matrix products, arithmetic and copies ran while one was open for 4% of the time, Pallas kernels for 0%

commit v1 on v0

--- a/solution.py
+++ b/solution.py
@@ -4,6 +4,22 @@
 from jax.sharding import PartitionSpec as P
 
 SLOT = 3
+
+
+def _change_trails(vals):
+    num_devices = lax.axis_size("local")
+    copies = tuple(((ix, (ix + 1) % num_devices) for ix in range(num_devices)))
+
+    def proceed_local_data(t_next):
+        if len(t_next) == num_devices:
+            return t_next
+        mixed_arr = lax.ppermute(t_next[0], "local", copies)
+        return proceed_local_data([mixed_arr, *t_next])
+
+    piece_now = proceed_local_data([vals])
+    out_arr = jnp.concatenate(piece_now, axis=0)
+    clean = lax.axis_index("local")
+    return jnp.roll(out_arr, (clean + 1) * vals.shape[0], axis=0)
 
 
 def shards(tokens, w_gate, w_up, w_down, chosen, counts, gates):
@@ -53,7 +69,7 @@
     down_mat = w_down[0]
     ff_dev = gate_mat.shape[1]
     arrived = lax.all_to_all(outgoing, "node", split_axis=0, concat_axis=0, tiled=True)
-    piece = lax.all_gather(arrived[None], "local", axis=0, tiled=True)
+    piece = _change_trails(arrived[None])
     flat = piece.reshape(-1, width)
     gate_val = jnp.dot(flat, gate_mat, preferred_element_type=jnp.float32)
     up_val = jnp.dot(flat, up_mat, preferred_element_type=jnp.float32)

time: 120 us -> 126 us (1.050)
  waiting for transfers between devices: 53.3 us -> 58.4 us
    ppermute x0 -> x3, waiting for transfers between devices: none -> 19.8 us  [proceed_local_data(): mixed_arr = lax.ppermute(t_next[0], 'local', copies)]
    all_gather x1 -> x0, waiting for transfers between devices: 13.7 us -> none  [shards(): piece = lax.all_gather(arrived[None], 'local', axis=0, tiled=True)]
    all_gather x1 -> x0, local copies, waits for them, and re-layouts: 3.75 us -> none  [shards(): piece = lax.all_gather(arrived[None], 'local', axis=0, tiled=True)]
    unnamed x6 -> x13, local copies, waits for them, and re-layouts: 0.24 us -> 3.58 us
    dynamic_slice x0 -> x1, local copies, waits for them, and re-layouts: none -> 1.91 us  [_change_trails(): return jnp.roll(out_arr, (clean + 1) * vals.shape[0], axis=0)]
  transfers between devices with their start and end apart: 3 -> 5, of which waited for: 3 -> 5; matrix products, arithmetic and copies ran while one was open for 4% -> 3% of each run, Pallas kernels for 0% -> 0%
where the time goes in v1:
time: 126 us
  waiting for transfers between devices  58.4 us (46%)
  blocking collectives  20.3 us (16%)
  local copies, waits for them, and re-layouts  14 us (11%)
  between operations  13.5 us (11%)
  matrix products  9.34 us (7%)
  starting transfers between devices  5.53 us (4%)
  other arithmetic  4.75 us (4%)
    reduce_scatter x1, waiting for transfers between devices, shards(): lax.psum_scatter(partial_value.astype(jnp.float32).astype(jnp.bfloat16),...  25.9 us
    all_to_all x1, blocking collectives, shards(): lax.all_to_all(outgoing, 'node', split_axis=0, concat_axis=0, tiled=True)  20.3 us
    ppermute x3, waiting for transfers between devices, proceed_local_data(): mixed_arr = lax.ppermute(t_next[0], 'local', copies)  19.8 us
    all_to_all x1, waiting for transfers between devices, shards(): lax.all_to_all(summed, 'node', split_axis=1, concat_axis=1, tiled=True)  12.7 us
    all_to_all x1, starting transfers between devices, shards(): lax.all_to_all(summed, 'node', split_axis=1, concat_axis=1, tiled=True)  5.52 us
    dot_general x1, matrix products, shards(): jnp.dot(down_hidden.reshape(-1, ff_dev), down_mat, preferred_element_type...  3.84 us
    unnamed x13, local copies, waits for them, and re-layouts  3.58 us
    reshape x1, local copies, waits for them, and re-layouts, shards(): flat = piece.reshape(-1, width)  2.97 us
  transfers between devices with their start and end apart: 5, of which 5 were waited for; matrix products, arithmetic and copies ran while one was open for 3% of the time, Pallas kernels for 0%

profile of v1, /device:TPU:0, one launch (start us, length us, event | category | flops | bytes accessed | tf_op | source)
XLA Modules:
  0.0 125.8 jit_solution(15514868085279137015)
XLA Ops:
  6.5 0.9 fusion.27
  7.6 0.7 multiply_subtract_fusion
  8.7 0.8 gather_fusion
  10.1 20.3 %all_to_all.10 = bf16[8,3,7168]{2,1,0:T(4,128)(2,1)S(1)} all-to-all(bf16[8,3,7168]{2,1,0:T(4,128)(2,1)S(1)} %broadcast_multiply_fusion), channel_id=1, replica_groups=mesh['node'=8,'local'=4] {'node'}, dimensions={0} | all-to-all | bytes 688128 | tf_op jit(solution)/shard_map/all_to_all | solution.py:71
  30.4 0.6 dynamic_slice.17
  31.0 0.7 and_select_fusion
  31.7 6.6 %collective-permute-done = bf16[1,8,3,7168]{3,2,1,0:T(4,128)(2,1)S(1)} collective-permute-done((bf16[1,8,3,7168]{3,2,1,0:T(4,128)(2,1)S(1)}, bf16[1,8,3,7168]{3,2,1,0:T(4,128)(2,1)S(1)}, u32[]{:S(2)}, u32[]{:S(2)}) %collective-permute-start) | collective-permute-done | bytes 344096 | tf_op jit(solution)/shard_map/ppermute | solution.py:16
  38.3 0.7 iota_compare_fusion.5
  39.3 6.9 %collective-permute-done.1 = bf16[1,8,3,7168]{3,2,1,0:T(4,128)(2,1)S(1)} collective-permute-done((bf16[1,8,3,7168]{3,2,1,0:T(4,128)(2,1)S(1)}, bf16[1,8,3,7168]{3,2,1,0:T(4,128)(2,1)S(1)}, u32[]{:S(2)}, u32[]{:S(2)}) %collective-permute-start.1) | collective-permute-done | bytes 344096 | tf_op jit(solution)/shard_map/ppermute | solution.py:16
  46.2 0.7 fusion.25
  46.9 0.7 add_add_fusion
  47.9 6.3 %collective-permute-done.2 = bf16[1,8,3,7168]{3,2,1,0:T(4,128)(2,1)} collective-permute-done((bf16[1,8,3,7168]{3,2,1,0:T(4,128)(2,1)S(1)}, bf16[1,8,3,7168]{3,2,1,0:T(4,128)(2,1)}, u32[]{:S(2)}, u32[]{:S(2)}) %collective-permute-start.2) | collective-permute-done | bytes 344096 | tf_op jit(solution)/shard_map/ppermute | solution.py:16
  54.2 1.2 constant_dynamic-update-slice_fusion.7
  56.0 1.2 constant_dynamic-update-slice_fusion.3
  57.8 1.9 %constant_dynamic-slice_fusion.2 = bf16[4,8,3,7168]{3,2,1,0:T(4,128)(2,1)} fusion(bf16[8,8,3,7168]{3,2,1,0:T(4,128)(2,1)S(1)} %constant_dynamic-update-slice_fusion, s32[]{:T(128)S(6)} %select_n.55), kind=kLoop, calls=%fused_computation.56 | loop fusion | bytes 2752516 | tf_op jit(solution)/shard_map/jit(_roll_dynamic)/dynamic_slice | solution.py:22
  59.7 3.0 %reshape.117 = bf16[96,7168]{1,0:T(8,128)(2,1)S(1)} reshape(bf16[4,8,3,7168]{3,2,1,0:T(4,128)(2,1)} %constant_dynamic-slice_fusion.2) | data formatting | bytes 2752512 | tf_op jit(solution)/shard_map/reshape | solution.py:73
  62.7 2.9 %fusion.4 = f32[96,256]{1,0:T(8,128)S(1)} fusion(bf16[96,7168]{1,0:T(8,128)(2,1)S(1)} %reshape.117, bf16[1,7168,256]{2,1,0:T(8,128)(2,1)} %param.8), kind=kOutput, calls=%fused_computation.7 | convolution fusion | flops 352321536 | bytes 5144576 | tf_op jit(solution)/shard_map/dot_general | solution.py:74
  65.8 0.7 fusion.9
  66.6 3.8 %fusion = bf16[4,8,3,7168]{3,1,2,0:T(8,128)(2,1)} fusion(bf16[1,256,7168]{2,1,0:T(8,128)(2,1)} %param.10, f32[4,8,3]{1,2,0:T(4,128)S(1)} %copy.21, bf16[4,8,3,256]{3,2,1,0:T(4,128)(2,1)S(1)} %dot_general.16), kind=kOutput, calls=%fused_computation.3 | convolution fusion | flops 353697792 | bytes 5095808 | tf_op jit(solution)/shard_map/dot_general | solution.py:79
  70.4 25.9 %reduce-scatter.2.cloned.1.call-done = bf16[1,8,3,7168]{3,1,2,0:T(8,128)(2,1)} async-done(((bf16[4,8,3,7168]{3,1,2,0:T(8,128)(2,1)}), bf16[1,8,3,7168]{3,1,2,0:T(8,128)(2,1)}) %reduce-scatter.2.cloned.1.call-update) | async-done | bytes 344080 | tf_op jit(solution)/shard_map/reduce_scatter | solution.py:84
  96.3 2.0 %copy.22 = bf16[1,8,3,7168]{3,2,0,1:T(4,128)(2,1)} copy(bf16[1,8,3,7168]{3,1,2,0:T(8,128)(2,1)} %reduce-scatter.2.cloned.1.call-done) | data formatting | bytes 688128 | tf_op jit(solution)/shard_map/reduce_scatter | solution.py:84
  98.4 5.5 %all-to-all-start.1 = ((bf16[1,8,3,7168]{3,2,0,1:T(4,128)(2,1)}), bf16[1,8,3,7168]{3,2,0,1:T(4,128)(2,1)S(1)}, u32[]{:S(2)}, u32[]{:S(2)}) async-start(bf16[1,8,3,7168]{3,2,0,1:T(4,128)(2,1)} %copy.22), calls=%async_computation.2 | async-start | bytes 917504 | tf_op jit(solution)/shard_map/all_to_all | solution.py:90
  104.2 12.7 %all-to-all-done.1 = bf16[1,8,3,7168]{3,2,0,1:T(4,128)(2,1)S(1)} async-done(((bf16[1,8,3,7168]{3,2,0,1:T(4,128)(2,1)}), bf16[1,8,3,7168]{3,2,0,1:T(4,128)(2,1)S(1)}, u32[]{:S(2)}, u32[]{:S(2)}) %all-to-all-start.1) | async-done | bytes 344096 | tf_op jit(solution)/shard_map/all_to_all | solution.py:90
  117.1 1.9 %convolution_convert_fusion = bf16[128,7168]{1,0:T(8,128)(2,1)} fusion(bf16[24,7168]{1,0:T(8,128)(2,1)S(1)} %reshape_squeeze.3, s32[24]{0:T(128)S(1)} %eq.69, pred[24]{0:T(512)(128)(4,1)S(1)} %gt.12), kind=kOutput, calls=%fused_computation.1 | convolution fusion | flops 44963840 | bytes 2179192 | tf_op jit(solution)/shard_map/dot_general | solution.py:95
  (39 shorter events, 3.8 us)
Async XLA Ops:
  6.5 2.2 %copy-start = (bf16[128,7168]{1,0:T(8,128)(2,1)S(1)}, bf16[128,7168]{1,0:T(8,128)(2,1)}, u32[]{:S(2)}) copy-start(bf16[128,7168]{1,0:T(8,128)(2,1)} %param.7) | copy-start | bytes 5505028
  6.5 23.8 %copy-start.2 = (s32[8]{0:T(128)S(1)}, s32[8]{0:T(128)}, u32[]{:S(2)}) copy-start(s32[8]{0:T(128)} %param.12) | copy-start | bytes 100
  6.5 89.8 %reduce-scatter.2.cloned.1.call-start = ((), (), s32[]{:S(2)}) async-start(), calls=%async_computation.3 | async-start | bytes 1720320 | tf_op jit(solution)/shard_map/reduce_scatter | solution.py:84
  30.4 7.9 %collective-permute-start = (bf16[1,8,3,7168]{3,2,1,0:T(4,128)(2,1)S(1)}, bf16[1,8,3,7168]{3,2,1,0:T(4,128)(2,1)S(1)}, u32[]{:S(2)}, u32[]{:S(2)}) collective-permute-start(bf16[1,8,3,7168]{3,2,1,0:T(4,128)(2,1)S(1)} %bitcast.37), channel_id=1, source_target_pairs={{0,1},{1,2},{2,3},{3,0},{4,5},{5,6},{6,7},{7,4},{8,9},{9,10},{10,1... | collective-permute-start | bytes 1032200 | tf_op jit(solution)/shard_map/ppermute | solution.py:16
  38.3 7.9 %collective-permute-start.1 = (bf16[1,8,3,7168]{3,2,1,0:T(4,128)(2,1)S(1)}, bf16[1,8,3,7168]{3,2,1,0:T(4,128)(2,1)S(1)}, u32[]{:S(2)}, u32[]{:S(2)}) collective-permute-start(bf16[1,8,3,7168]{3,2,1,0:T(4,128)(2,1)S(1)} %collective-permute-done), channel_id=1, source_target_pairs={{0,1},{1,2},{2,3},{3,0},{4,5},{5,6},{6,7},{7,4},{8,9},{9,10},{10,1... | collective-permute-start | bytes 1032200 | tf_op jit(solution)/shard_map/ppermute | solution.py:16
  46.2 8.0 %collective-permute-start.2 = (bf16[1,8,3,7168]{3,2,1,0:T(4,128)(2,1)S(1)}, bf16[1,8,3,7168]{3,2,1,0:T(4,128)(2,1)}, u32[]{:S(2)}, u32[]{:S(2)}) collective-permute-start(bf16[1,8,3,7168]{3,2,1,0:T(4,128)(2,1)S(1)} %collective-permute-done.1), channel_id=1, source_target_pairs={{0,1},{1,2},{2,3},{3,0},{4,5},{5,6},{6,7},{7,4},{8,9},{9,10},{10,1... | collective-permute-start | bytes 1032200 | tf_op jit(solution)/shard_map/ppermute | solution.py:16
  62.6 3.1 %copy-start.1 = (bf16[1,7168,256]{2,1,0:T(8,128)(2,1)S(1)}, bf16[1,7168,256]{2,1,0:T(8,128)(2,1)}, u32[]{:S(2)}) copy-start(bf16[1,7168,256]{2,1,0:T(8,128)(2,1)} %param.9) | copy-start | bytes 11010052
  98.4 18.5 %all-to-all-start.1 = ((bf16[1,8,3,7168]{3,2,0,1:T(4,128)(2,1)}), bf16[1,8,3,7168]{3,2,0,1:T(4,128)(2,1)S(1)}, u32[]{:S(2)}, u32[]{:S(2)}) async-start(bf16[1,8,3,7168]{3,2,0,1:T(4,128)(2,1)} %copy.22), calls=%async_computation.2 | async-start | bytes 917504 | tf_op jit(solution)/shard_map/all_to_all | solution.py:90
Sparse Core Ops, SparseCore 0:
  70.5 25.7 reduce-scatter.1
